TPU v7x, 32 devices: a whole 2x2x4 slice. The times are simulated.
32 devices in a mesh: net: 4 (over y, x), line: 8 (over z, core).
Axes of the slice: x: 2, y: 2, z: 4, core: 2. Of those that a mesh axis runs over, the one named last changes fastest.
Arguments:
- conductance_inverse: float32 [4, 4096, 4096], P('net', 'line'), may hold values from -0.5 to 4.5, as said below
- prior_voltage: float32 [4, 96, 4096], P('net', None, 'line'), may hold values from -6 to 6
- sources: float32 [3, 4, 4096], P(None, 'net', 'line'), may hold values from -6 to 6
- fault_node: int32 [96], replicated, may hold values from 0 to 16383
- fault_conductance: float32 [96], replicated, may hold values from 0.5 to 4
- terminal_node: int32 [4, 3, 4096], P('net', None, 'line'), may hold values from 0 to 4095
- ownership: int32 [4, 4096], P('net', 'line'), may hold values from 0 to 1, as said below
- partner: int32 [4, 4096], P('net', 'line'), may hold values from 0 to 31, as said below
- delay_steps: int32 [4, 4096], P('net', 'line'), may hold values from 1 to 4, as said below
- surge_conductance: float32 [4, 4096], P('net', 'line'), may hold values from 0.2 to 1
- pole_wave: float32 [4, 6, 4096], P('net', None, 'line'), may hold values from 0.2 to 0.95
- residue_wave: float32 [4, 6, 3, 3, 4096], P('net', None, None, None, 'line'), may hold values from -1 to 1
- pole_admit: float32 [4, 6, 4096], P('net', None, 'line'), may hold values from 0.2 to 0.95
- residue_admit: float32 [4, 6, 3, 3, 4096], P('net', None, None, None, 'line'), may hold values from -1 to 1
- wave_state: float32 [4, 6, 3, 96, 4096], P('net', None, None, None, 'line'), may hold values from -4 to 4
- admit_state: float32 [4, 6, 3, 96, 4096], P('net', None, None, None, 'line'), may hold values from -4 to 4
- wave_history: float32 [4, 4, 3, 96, 4096], P('net', None, None, None, 'line'), may hold values from -6 to 6
Outputs:
- final_voltage: float32 [4, 96, 4096], P('net', None, 'line')
- end_current: float32 [4, 3, 96, 4096], P('net', None, None, 'line')
Inputs may be any that keep to these rules, and one draw needn't show every extreme that they name: `conductance_inverse`: each block is exactly symmetric. `ownership`: A slot is live exactly when the slot of the same number j % 512 at its partner owner is live; the number of live slots differs from owner to owner. The far end of slot j lies in the slot of the same number j % 512 at the partner owner, the partner of that slot is the first owner again, never the owner itself, and at most 17 live slots of one owner have the same partner; this many occur. `delay_steps`: equal at both ends of a line.
All inputs are finite; a program needn't handle non-finite values.
Results may differ from a plain program's by a relative error of at most 0.0003.
Values sent between devices are 32-bit elements; how exact they have to be, the bound alone decides.
A program may use at most 128 MiB of HBM per device.

v0:
```python
import jax
import jax.numpy as jnp
from jax import lax
from jax.sharding import PartitionSpec as P

STEPS = 3


def mix_residue(residue, vector):
    return (
        residue[:, :, 0, None, :] * vector[0]
        + residue[:, :, 1, None, :] * vector[1]
        + residue[:, :, 2, None, :] * vector[2]
    )


def select_delayed(buffer, delay_local):
    depth_count = buffer.shape[0]
    chosen = delay_local[None, :] == jnp.arange(1, depth_count + 1, dtype=jnp.int32)[:, None]
    return jnp.sum(jnp.where(chosen[:, None, None, :], buffer, 0.0), axis=0)


def terminal_values(voltage, terminal):
    picked = jnp.take(voltage, terminal.reshape(-1), axis=1)
    return jnp.moveaxis(picked.reshape(voltage.shape[0], 3, -1), 0, 1)


def spread_ends(history, terminal, node_count):
    values = jnp.moveaxis(history, 0, 1).reshape(history.shape[1], -1)
    return (
        jnp.zeros((history.shape[1], node_count), jnp.float32)
        .at[:, terminal.reshape(-1)]
        .add(values)
    )


def gather_full(block):
    return lax.all_gather(block, "line", axis=1, tiled=True)


def on_device(
    conductance_inverse,
    prior_voltage,
    sources,
    fault_node,
    fault_conductance,
    terminal_node,
    ownership,
    partner,
    delay_steps,
    surge_conductance,
    pole_wave,
    residue_wave,
    pole_admit,
    residue_admit,
    wave_state,
    admit_state,
    wave_history,
):
    inverse_block = conductance_inverse[0]
    row_count = inverse_block.shape[0]
    node_count = inverse_block.shape[1]
    line_index = lax.axis_index("line")
    net_index = lax.axis_index("net")
    offset = line_index * row_count
    net_count = lax.axis_size("net")
    line_count = lax.axis_size("line")
    devices = net_count * line_count
    slot_count = ownership.shape[1]
    capacity = (slot_count + devices - 2) // (devices - 1)
    is_live = ownership[0] > 0
    live_float = is_live.astype(jnp.float32)
    terminal = terminal_node[0]
    delay_local = delay_steps[0]
    surge_local = surge_conductance[0]
    partners = partner[0]
    slot_range = jnp.arange(slot_count, dtype=jnp.int32)
    earlier = (
        (partners[:, None] == partners[None, :])
        & is_live[None, :]
        & (slot_range[None, :] < slot_range[:, None])
    )
    slot_rank = jnp.sum(earlier.astype(jnp.int32), axis=1)
    position = jnp.where(is_live, partners * capacity + slot_rank, devices * capacity)
    scenario_range = jnp.arange(prior_voltage.shape[1], dtype=jnp.int32)
    fault_sub = fault_node // node_count
    fault_local = fault_node % node_count
    fault_here = (fault_sub == net_index) & (fault_local // row_count == line_index)
    wave_decay = pole_wave[0][:, None, None, :]
    admit_decay = pole_admit[0][:, None, None, :]
    wave_res = residue_wave[0]
    admit_res = residue_admit[0]
    voltage = gather_full(prior_voltage[0])
    voltage_rows = prior_voltage[0]
    wave_now = wave_state[0]
    admits = admit_state[0]
    history_buffer = wave_history[0]
    outgoing = None
    current = None
    for step_index in range(STEPS):
        terminal_prior = terminal_values(voltage, terminal)
        admits = admit_decay * admits + mix_residue(admit_res, terminal_prior)
        if step_index == 0:
            wave_now = wave_decay * wave_now + mix_residue(
                wave_res, select_delayed(history_buffer, delay_local)
            )
        else:
            shifted = jnp.concatenate(
                [jnp.zeros_like(history_buffer[:1]), history_buffer[:-1]], axis=0
            )
            wave_now = wave_decay * wave_now + mix_residue(
                wave_res, select_delayed(shifted, delay_local)
            )
            row_width = outgoing.shape[0] * outgoing.shape[1]
            packed = jnp.moveaxis(outgoing, 2, 0).reshape(slot_count, row_width)
            buffer = (
                jnp.zeros((devices * capacity, row_width), jnp.float32)
                .at[position]
                .set(packed, mode="drop")
            )
            arrived = lax.all_to_all(
                buffer, ("net", "line"), split_axis=0, concat_axis=0, tiled=True
            )
            picked_rows = arrived[jnp.minimum(position, devices * capacity - 1)]
            arrived = jnp.moveaxis(picked_rows.reshape(slot_count, 3, -1), 0, 2) * live_float
            newest = jnp.where((delay_local == 1)[None, None, :], arrived, 0.0)
            wave_now = wave_now + mix_residue(wave_res, newest)
            history_buffer = jnp.concatenate([arrived[None], shifted[1:]], axis=0)
        history = (jnp.sum(wave_now, axis=0) - jnp.sum(admits, axis=0)) * live_float
        injection = spread_ends(history, terminal, node_count)
        own_part = (
            lax.dynamic_slice_in_dim(injection, offset, row_count, 1)
            + sources[step_index, 0][None, :]
        )
        injection = lax.dynamic_update_slice_in_dim(injection, own_part, offset, 1)
        fault_value = voltage[scenario_range, fault_local]
        injection = injection.at[scenario_range, fault_local].add(
            jnp.where(fault_here, -fault_conductance * fault_value, 0.0)
        )
        summed = lax.psum(injection, "line")
        voltage_rows = lax.dot_general(
            summed,
            inverse_block,
            (((1,), (1,)), ((), ())),
            precision=lax.Precision.HIGHEST,
            preferred_element_type=jnp.float32,
        )
        voltage = gather_full(voltage_rows)
        terminal_now = terminal_values(voltage, terminal)
        if step_index + 1 < STEPS:
            outgoing = (2.0 * surge_local * terminal_now - history) * live_float
        else:
            current = (surge_local * terminal_now - history) * live_float
    return (voltage_rows[None], current[None])


def solution(mesh):
    return jax.shard_map(
        on_device,
        mesh=mesh,
        in_specs=(
            P("net", "line", None),
            P("net", None, "line"),
            P(None, "net", "line"),
            P(),
            P(),
            P("net", None, "line"),
            P("net", "line"),
            P("net", "line"),
            P("net", "line"),
            P("net", "line"),
            P("net", None, "line"),
            P("net", None, None, None, "line"),
            P("net", None, "line"),
            P("net", None, None, None, "line"),
            P("net", None, None, None, "line"),
            P("net", None, None, None, "line"),
            P("net", None, None, None, "line"),
        ),
        out_specs=(P("net", None, "line"), P("net", None, None, "line")),
        check_vma=False,
    )
```

profile of v0, /device:TPU:0, one launch (start us, length us, event | category | flops | bytes accessed | tf_op | source)
XLA Modules:
  0.0 577.8 jit_solution(13432879487147559588)
XLA Ops:
  32.9 8.7 %all-gather.12.cloned.1.call-done = f32[1,96,4096]{1,2,0:T(8,128)} async-done(((f32[1,96,512]{1,2,0:T(8,128)}), f32[1,96,4096]{1,2,0:T(8,128)}) %all-gather.12.cloned.1.call-update) | async-done | bytes 1572880 | tf_op jit(solution)/shard_map/all_gather | solution.py:38
  41.5 3.6 gather_fusion
  45.1 5.6 gather_fusion.5
  64.7 10.5 %scatter_custom_fusion = f32[96,4096]{0,1:T(8,128)} fusion(s32[1536]{0:T(1024)} %fusion.32, f32[1536,96]{1,0:T(8,128)} %copy.74, f32[]{:T(128)} %constant.37.clone.1), kind=kCustom, calls=%fused_computation.47 | custom fusion | flops 147456 | bytes 1573376 | tf_op jit(solution)/shard_map/scatter-add | solution.py:33
  81.1 12.2 %scatter_fusion = f32[96,4096]{1,0:T(8,128)} fusion(f32[96,4096]{1,0:T(8,128)} %copy.75, s32[96]{0:T(128)S(1)} %fusion.36, f32[96]{0:T(128)} %get-tuple-element.9), kind=kCustom, calls=%fused_computation.10 | custom fusion | flops 96 | bytes 1920 | tf_op jit(solution)/shard_map/scatter-add | solution.py:137
  93.6 61.2 %all-reduce.6.cloned.1.call-done = f32[96,4096]{1,0:T(8,128)} async-done(((f32[96,4096]{1,0:T(8,128)}), f32[96,4096]{1,0:T(8,128)}) %all-reduce.6.cloned.1.call-update) | async-done | bytes 1572880 | tf_op jit(solution)/shard_map/psum | solution.py:140
  154.8 12.7 %fusion.4 = f32[96,512]{1,0:T(8,128)} fusion(f32[96,4096]{1,0:T(8,128)} %all-reduce.6.cloned.1.call-done, f32[1,512,4096]{2,1,0:T(8,128)} %param.19), kind=kOutput, calls=%fused_computation.21 | convolution fusion | flops 2415919104 | bytes 10158080 | tf_op jit(solution)/shard_map/dot_general | solution.py:141
  174.4 17.7 %all-gather.6.cloned.1.call-done = f32[96,4096]{1,0:T(8,128)} async-done(((f32[96,512]{1,0:T(8,128)}), f32[96,4096]{1,0:T(8,128)}) %all-gather.6.cloned.1.call-update) | async-done | bytes 1572880 | tf_op jit(solution)/shard_map/all_gather | solution.py:38
  194.9 5.6 gather_fusion.6
  209.6 3.7 scatter_custom_fusion.2
  215.7 3.8 all-to-all-start
  229.6 3.5 gather_fusion.2
  234.3 4.2 fusion.11
  238.5 11.3 %all-to-all-done = f32[32,17,288]{2,1,0:T(8,128)} async-done(((f32[32,17,288]{2,1,0:T(8,128)}), f32[32,17,288]{2,1,0:T(8,128)}, u32[]{:S(2)}, u32[]{:S(2)}) %all-to-all-start) | async-done | bytes 626720 | tf_op jit(solution)/shard_map/all_to_all | solution.py:121
  256.8 3.9 fusion.38
  262.1 9.4 %scatter_custom_fusion.3 = f32[96,4096]{0,1:T(8,128)S(1)} fusion(s32[1536]{0:T(1024)} %fusion.32, f32[1536,96]{1,0:T(8,128)S(1)} %copy.84, f32[]{:T(128)} %constant.37.clone.1), kind=kCustom, calls=%fused_computation.45 | custom fusion | flops 147456 | bytes 1573376 | tf_op jit(solution)/shard_map/scatter-add | solution.py:33
  273.3 12.2 %scatter_fusion.1 = f32[96,4096]{1,0:T(8,128)} fusion(f32[96,4096]{1,0:T(8,128)} %copy.85, s32[96]{0:T(128)S(1)} %fusion.36, f32[96]{0:T(128)S(1)} %copy-done.45), kind=kCustom, calls=%fused_computation.13 | custom fusion | flops 96 | bytes 1920 | tf_op jit(solution)/shard_map/scatter-add | solution.py:137
  286.0 59.3 %all-reduce.8.cloned.1.call-done = f32[96,4096]{1,0:T(8,128)} async-done(((f32[96,4096]{1,0:T(8,128)}), f32[96,4096]{1,0:T(8,128)}) %all-reduce.8.cloned.1.call-update) | async-done | bytes 1572880 | tf_op jit(solution)/shard_map/psum | solution.py:140
  345.3 12.6 %fusion.2 = f32[96,512]{1,0:T(8,128)} fusion(f32[96,4096]{1,0:T(8,128)} %all-reduce.8.cloned.1.call-done, f32[1,512,4096]{2,1,0:T(8,128)} %param.19), kind=kOutput, calls=%fused_computation.19 | convolution fusion | flops 2415919104 | bytes 10158080 | tf_op jit(solution)/shard_map/dot_general | solution.py:141
  358.8 23.8 %all-gather.8.cloned.1.call-done = f32[96,4096]{1,0:T(8,128)} async-done(((f32[96,512]{1,0:T(8,128)}), f32[96,4096]{1,0:T(8,128)}) %all-gather.8.cloned.1.call-update) | async-done | bytes 1572880 | tf_op jit(solution)/shard_map/all_gather | solution.py:38
  384.5 3.7 gather_fusion.7
  390.5 3.3 scatter_custom_fusion.5
  396.3 3.8 all-to-all-start.1
  407.6 3.5 gather_fusion.4
  412.3 4.8 add_reduce_fusion
  417.2 13.2 %all-to-all-done.1 = f32[32,17,288]{2,1,0:T(8,128)} async-done(((f32[32,17,288]{2,1,0:T(8,128)}), f32[32,17,288]{2,1,0:T(8,128)}, u32[]{:S(2)}, u32[]{:S(2)}) %all-to-all-start.1) | async-done | bytes 626720 | tf_op jit(solution)/shard_map/all_to_all | solution.py:121
  442.0 9.4 %scatter_custom_fusion.6 = f32[96,4096]{0,1:T(8,128)S(1)} fusion(s32[1536]{0:T(1024)} %fusion.32, f32[1536,96]{1,0:T(8,128)S(1)} %copy.94, f32[]{:T(128)} %constant.37.clone.1), kind=kCustom, calls=%fused_computation.43 | custom fusion | flops 147456 | bytes 1573376 | tf_op jit(solution)/shard_map/scatter-add | solution.py:33
  453.2 12.2 %scatter_fusion.2 = f32[96,4096]{1,0:T(8,128)} fusion(f32[96,4096]{1,0:T(8,128)} %copy.95, s32[96]{0:T(128)S(1)} %fusion.36, f32[96]{0:T(128)S(1)} %copy-done.44), kind=kCustom, calls=%fused_computation.16 | custom fusion | flops 96 | bytes 1920 | tf_op jit(solution)/shard_map/scatter-add | solution.py:137
  465.7 59.5 %all-reduce.10.cloned.1.call-done = f32[96,4096]{1,0:T(8,128)} async-done(((f32[96,4096]{1,0:T(8,128)}), f32[96,4096]{1,0:T(8,128)}) %all-reduce.10.cloned.1.call-update) | async-done | bytes 1572880 | tf_op jit(solution)/shard_map/psum | solution.py:140
  525.2 12.7 %fusion = f32[96,512]{1,0:T(8,128)} fusion(f32[96,4096]{1,0:T(8,128)} %all-reduce.10.cloned.1.call-done, f32[1,512,4096]{2,1,0:T(8,128)} %param.19), kind=kOutput, calls=%fused_computation.17 | convolution fusion | flops 2415919104 | bytes 10158080 | tf_op jit(solution)/shard_map/dot_general | solution.py:141
  537.9 24.6 %all-gather.10.cloned.1.call-done = f32[96,4096]{1,0:T(8,128)} async-done(((f32[96,512]{1,0:T(8,128)}), f32[96,4096]{1,0:T(8,128)}) %all-gather.10.cloned.1.call-update) | async-done | bytes 1572880 | tf_op jit(solution)/shard_map/all_gather | solution.py:38
  564.4 3.7 gather_fusion.8
  (207 shorter events, 122.7 us)
Async XLA Ops:
  7.2 18.5 %copy-start.46 = (s32[96]{0:T(128)S(1)}, s32[96]{0:T(128)}, u32[]{:S(2)}) copy-start(s32[96]{0:T(128)} %param.22) | copy-start | bytes 1156
  7.2 23.8 %copy-start.2 = (f32[1,6,3,96,512]{4,3,2,1,0:T(8,128)S(1)}, f32[1,6,3,96,512]{4,3,2,1,0:T(8,128)}, u32[]{:S(2)}) copy-start(f32[1,6,3,96,512]{4,3,2,1,0:T(8,128)} %param.33) | copy-start | bytes 10616836
  7.2 34.3 %all-gather.12.cloned.1.call-start = ((), (), s32[]{:S(2)}) async-start(), calls=%async_computation.8 | async-start | bytes 2359296 | tf_op jit(solution)/shard_map/all_gather | solution.py:38
  9.2 145.6 %all-reduce.6.cloned.1.call-start = ((), (), s32[]{:S(2)}) async-start(), calls=%async_computation.2 | async-start | bytes 3145728 | tf_op jit(solution)/shard_map/psum | solution.py:140
  12.5 11.2 %copy-start.35 = (s32[1536]{0:T(1024)}, s32[1536]{0:T(1024)S(1)}, u32[]{:S(2)}) copy-start(s32[1536]{0:T(1024)S(1)} %reshape_squeeze.5) | copy-start | bytes 18436
  20.2 10.8 %copy-start.25 = (f32[6,3,1,512]{3,1,2,0:T(4,128)S(1)}, f32[6,3,1,512]{3,1,2,0:T(4,128)}, u32[]{:S(2)}) copy-start(f32[6,3,1,512]{3,1,2,0:T(4,128)} %copy.124) | copy-start | bytes 110596
  20.2 10.8 %copy-start.31 = (f32[1,6,512]{2,1,0:T(8,128)S(1)}, f32[1,6,512]{2,1,0:T(8,128)}, u32[]{:S(2)}) copy-start(f32[1,6,512]{2,1,0:T(8,128)} %copy.126) | copy-start | bytes 36868
  23.6 4.2 copy-start.36
  50.7 7.7 %copy-start = (f32[1,6,3,96,512]{4,3,2,1,0:T(8,128)S(1)}, f32[1,6,3,96,512]{4,3,2,1,0:T(8,128)}, u32[]{:S(2)}) copy-start(f32[1,6,3,96,512]{4,3,2,1,0:T(8,128)} %param.34) | copy-start | bytes 10616836
  93.4 98.7 %all-gather.6.cloned.1.call-start = ((), (), s32[]{:S(2)}) async-start(), calls=%async_computation.3 | async-start | bytes 1769472 | tf_op jit(solution)/shard_map/all_gather | solution.py:38
  215.7 34.1 %all-to-all-start = ((f32[32,17,288]{2,1,0:T(8,128)}), f32[32,17,288]{2,1,0:T(8,128)}, u32[]{:S(2)}, u32[]{:S(2)}) async-start(f32[32,17,288]{2,1,0:T(8,128)} %all_to_all.16), calls=%async_computation | async-start | bytes 2359296 | tf_op jit(solution)/shard_map/all_to_all | solution.py:121
  219.5 125.8 %all-reduce.8.cloned.1.call-start = ((), (), s32[]{:S(2)}) async-start(), calls=%async_computation.4 | async-start | bytes 3145728 | tf_op jit(solution)/shard_map/psum | solution.py:140
  256.8 4.8 copy-start.14
  260.8 10.7 %copy-start.41 = (f32[1,1,512]{2,1,0:T(1,128)S(1)}, f32[1,1,512]{2,1,0:T(1,128)}, u32[]{:S(2)}) copy-start(f32[1,1,512]{2,1,0:T(1,128)} %get-tuple-element.45) | copy-start | bytes 6148
  261.8 11.6 %copy-start.45 = (f32[96]{0:T(128)S(1)}, f32[96]{0:T(128)}, u32[]{:S(2)}) copy-start(f32[96]{0:T(128)} %multiply_select_fusion.1) | copy-start | bytes 1156
  285.6 72.4 %copy-start.18 = (f32[3,96,512]{2,1,0:T(8,128)S(1)}, f32[3,96,512]{2,1,0:T(8,128)}, u32[]{:S(2)}) copy-start(f32[3,96,512]{2,1,0:T(8,128)} %get-tuple-element.3) | copy-start | bytes 1769476
  285.6 97.0 %all-gather.8.cloned.1.call-start = ((), (), s32[]{:S(2)}) async-start(), calls=%async_computation.5 | async-start | bytes 1769472 | tf_op jit(solution)/shard_map/all_gather | solution.py:38
  358.0 26.5 %copy-start.33 = (s32[2048]{0:T(1024)S(1)}, s32[2048]{0:T(1024)}, u32[]{:S(2)}) copy-start(s32[2048]{0:T(1024)} %pad_clamp_fusion) | copy-start | bytes 24580
  384.4 5.4 copy-start.11
  384.5 5.4 copy-start.15
  384.5 5.4 copy-start.38
  393.8 18.5 %copy-start.1 = (f32[1,6,3,96,512]{4,3,2,1,0:T(8,128)S(1)}, f32[1,6,3,96,512]{4,3,2,1,0:T(8,128)}, u32[]{:S(2)}) copy-start(f32[1,6,3,96,512]{4,3,2,1,0:T(8,128)} %param.34) | copy-start | bytes 10616836
  396.3 34.1 %all-to-all-start.1 = ((f32[32,17,288]{2,1,0:T(8,128)}), f32[32,17,288]{2,1,0:T(8,128)}, u32[]{:S(2)}, u32[]{:S(2)}) async-start(f32[32,17,288]{2,1,0:T(8,128)} %all_to_all.19), calls=%async_computation.1 | async-start | bytes 2359296 | tf_op jit(solution)/shard_map/all_to_all | solution.py:121
  400.1 125.1 %all-reduce.10.cloned.1.call-start = ((), (), s32[]{:S(2)}) async-start(), calls=%async_computation.6 | async-start | bytes 3145728 | tf_op jit(solution)/shard_map/psum | solution.py:140
  431.8 4.8 copy-start.42
  440.8 10.5 %copy-start.40 = (f32[1,1,512]{2,1,0:T(1,128)S(1)}, f32[1,1,512]{2,1,0:T(1,128)}, u32[]{:S(2)}) copy-start(f32[1,1,512]{2,1,0:T(1,128)} %get-tuple-element.43) | copy-start | bytes 6148
  441.7 11.5 %copy-start.44 = (f32[96]{0:T(128)S(1)}, f32[96]{0:T(128)}, u32[]{:S(2)}) copy-start(f32[96]{0:T(128)} %multiply_select_fusion) | copy-start | bytes 1156
  465.5 97.0 %all-gather.10.cloned.1.call-start = ((), (), s32[]{:S(2)}) async-start(), calls=%async_computation.7 | async-start | bytes 1769472 | tf_op jit(solution)/shard_map/all_gather | solution.py:38
  537.9 26.5 %copy-start.34 = (s32[2048]{0:T(1024)S(1)}, s32[2048]{0:T(1024)}, u32[]{:S(2)}) copy-start(s32[2048]{0:T(1024)} %pad_clamp_fusion) | copy-start | bytes 24580
  564.4 5.4 copy-start.8
  564.4 5.4 copy-start.17
  564.4 5.4 copy-start.39
  (25 other events, 47.3 us)
Sparse Core Ops, SparseCore 0:
  9.6 31.8 all-gather.11
  93.5 61.2 all-reduce.5
  167.6 24.4 all-gather.5
  285.7 59.5 all-reduce.7
  358.1 24.4 all-gather.7
  465.6 59.5 all-reduce.9
  538.0 24.4 all-gather.9
where the time goes:
time: 587 us; the launch traced here: 578 us
  waiting for transfers between devices  279 us (48%)
  other arithmetic  122 us (21%)
  local copies, waits for them, and re-layouts  115 us (20%)
  matrix products  38 us (6%)
  between operations  15.2 us (3%)
  starting transfers between devices  9.15 us (2%)
    psum x3, waiting for transfers between devices, on_device(): summed = lax.psum(injection, 'line')  180 us
    all_gather x4, waiting for transfers between devices, gather_full(): return lax.all_gather(block, 'line', axis=1, tiled=True)  74.8 us
    dot_general x3, matrix products, on_device(): lax.dot_general(summed, inverse_block, (((1,), (1,)), ((), ())), precisio...  38 us
    scatter-add x3, other arithmetic, on_device(): injection.at[scenario_range, fault_local]  36.6 us
    scatter-add x3, other arithmetic, spread_ends(): return jnp.zeros((history.shape[1], node_count), jnp.float32).at[:, termi...  29.3 us
    all_to_all x2, waiting for transfers between devices, on_device(): lax.all_to_all(buffer, ('net', 'line'), split_axis=0, concat_axis=0, tile...  24.6 us
    reduce_sum x6, other arithmetic, on_device(): history = (jnp.sum(wave_now, axis=0) - jnp.sum(admits, axis=0)) * live_float  20.3 us
    gather x4, local copies, waits for them, and re-layouts, terminal_values(): picked = jnp.take(voltage, terminal.reshape(-1), axis=1)  18.5 us
  transfers between devices with their start and end apart: 9, of which 9 were waited for; matrix products, arithmetic and copies ran while one was open for 11% of the time, Pallas kernels for 0%

commit v1 on v0

--- a/solution.py
+++ b/solution.py
@@ -137,7 +137,9 @@
         injection = injection.at[scenario_range, fault_local].add(
             jnp.where(fault_here, -fault_conductance * fault_value, 0.0)
         )
-        summed = lax.psum(injection, "line")
+        summed = injection
+        for hop in (1, 2, 4):
+            summed = summed + lax.ppermute(summed, "line", [(dev, dev ^ hop) for dev in range(8)])
         voltage_rows = lax.dot_general(
             summed,
             inverse_block,

time: 587 us -> 735 us (1.25)
  waiting for transfers between devices: 279 us -> 424 us
    ppermute x0 -> x9, waiting for transfers between devices: none -> 327 us  [on_device(): lax.ppermute(summed, 'line', [(dev, dev ^ hop) for dev in range(8)])]
    psum x3 -> x0, waiting for transfers between devices: 180 us -> none  [on_device(): summed = lax.psum(injection, 'line')]
  transfers between devices with their start and end apart: 9 -> 15, of which waited for: 9 -> 15; matrix products, arithmetic and copies ran while one was open for 11% -> 9% of each run, Pallas kernels for 0% -> 0%
where the time goes in v1:
time: 735 us; the launch traced here: 726 us
  waiting for transfers between devices  424 us (58%)
  other arithmetic  127 us (17%)
  local copies, waits for them, and re-layouts  115 us (16%)
  matrix products  33.6 us (5%)
  between operations  15.1 us (2%)
  starting transfers between devices  12.2 us (2%)
    ppermute x9, waiting for transfers between devices, on_device(): lax.ppermute(summed, 'line', [(dev, dev ^ hop) for dev in range(8)])  327 us
    all_gather x4, waiting for transfers between devices, gather_full(): return lax.all_gather(block, 'line', axis=1, tiled=True)  71.8 us
    scatter-add x3, other arithmetic, on_device(): injection.at[scenario_range, fault_local]  36.7 us
    dot_general x3, matrix products, on_device(): lax.dot_general(summed, inverse_block, (((1,), (1,)), ((), ())), precisio...  33.6 us
    scatter-add x3, other arithmetic, spread_ends(): return jnp.zeros((history.shape[1], node_count), jnp.float32).at[:, termi...  30.5 us
    all_to_all x2, waiting for transfers between devices, on_device(): lax.all_to_all(buffer, ('net', 'line'), split_axis=0, concat_axis=0, tile...  24.5 us
    reduce_sum x6, other arithmetic, on_device(): history = (jnp.sum(wave_now, axis=0) - jnp.sum(admits, axis=0)) * live_float  20.3 us
    gather x4, local copies, waits for them, and re-layouts, terminal_values(): picked = jnp.take(voltage, terminal.reshape(-1), axis=1)  18.5 us
  transfers between devices with their start and end apart: 15, of which 15 were waited for; matrix products, arithmetic and copies ran while one was open for 9% of the time, Pallas kernels for 0%

profile of v1, /device:TPU:0, one launch (start us, length us, event | category | flops | bytes accessed | tf_op | source)
XLA Modules:
  0.0 726.3 jit_solution(3643741070859684946)
XLA Ops:
  32.9 8.6 %all-gather.12.cloned.1.call-done = f32[1,96,4096]{1,2,0:T(8,128)} async-done(((f32[1,96,512]{1,2,0:T(8,128)}), f32[1,96,4096]{1,2,0:T(8,128)}) %all-gather.12.cloned.1.call-update) | async-done | bytes 1572880 | tf_op jit(solution)/shard_map/all_gather | solution.py:38
  45.1 5.6 gather_fusion.5
  64.8 11.0 %scatter_custom_fusion = f32[96,4096]{0,1:T(8,128)} fusion(s32[1536]{0:T(1024)} %fusion.35, f32[1536,96]{1,0:T(8,128)} %copy.74, f32[]{:T(128)} %constant.37.clone.1), kind=kCustom, calls=%fused_computation.50 | custom fusion | flops 147456 | bytes 1573376 | tf_op jit(solution)/shard_map/scatter-add | solution.py:33
  81.6 12.2 %scatter_fusion = f32[96,4096]{1,0:T(8,128)} fusion(f32[96,4096]{1,0:T(8,128)} %copy.75, s32[96]{0:T(128)S(1)} %fusion.39, f32[96]{0:T(128)} %get-tuple-element.9), kind=kCustom, calls=%fused_computation.10 | custom fusion | flops 96 | bytes 1920 | tf_op jit(solution)/shard_map/scatter-add | solution.py:137
  100.6 35.1 %collective-permute-done.1 = f32[96,4096]{1,0:T(8,128)S(1)} collective-permute-done((f32[96,4096]{1,0:T(8,128)S(1)}, f32[96,4096]{1,0:T(8,128)S(1)}, u32[]{:S(2)}, u32[]{:S(2)}) %collective-permute-start.1) | collective-permute-done | bytes 1572896 | tf_op jit(solution)/shard_map/ppermute | solution.py:142
  137.7 68.5 %collective-permute-done.2 = f32[96,4096]{1,0:T(8,128)S(1)} collective-permute-done((f32[96,4096]{1,0:T(8,128)S(1)}, f32[96,4096]{1,0:T(8,128)S(1)}, u32[]{:S(2)}, u32[]{:S(2)}) %collective-permute-start.2) | collective-permute-done | bytes 1572896 | tf_op jit(solution)/shard_map/ppermute | solution.py:142
  206.2 11.2 %fusion.4 = f32[96,512]{1,0:T(8,128)} fusion(f32[1,512,4096]{2,1,0:T(8,128)} %param.19, f32[96,4096]{1,0:T(8,128)S(1)} %add.258, f32[96,4096]{1,0:T(8,128)S(1)} %collective-permute-done.2), kind=kOutput, calls=%fused_computation.21 | convolution fusion | flops 2416312320 | bytes 11730944 | tf_op jit(solution)/shard_map/dot_general | solution.py:143
  224.4 17.8 %all-gather.6.cloned.1.call-done = f32[96,4096]{1,0:T(8,128)} async-done(((f32[96,512]{1,0:T(8,128)}), f32[96,4096]{1,0:T(8,128)}) %all-gather.6.cloned.1.call-update) | async-done | bytes 1572880 | tf_op jit(solution)/shard_map/all_gather | solution.py:38
  245.0 5.6 gather_fusion.6
  259.7 3.7 scatter_custom_fusion.2
  265.8 3.8 all-to-all-start
  284.3 4.2 fusion.11
  288.5 11.4 %all-to-all-done = f32[32,17,288]{2,1,0:T(8,128)} async-done(((f32[32,17,288]{2,1,0:T(8,128)}), f32[32,17,288]{2,1,0:T(8,128)}, u32[]{:S(2)}, u32[]{:S(2)}) %all-to-all-start) | async-done | bytes 626720 | tf_op jit(solution)/shard_map/all_to_all | solution.py:121
  305.8 3.9 fusion.41
  311.1 9.8 %scatter_custom_fusion.3 = f32[96,4096]{0,1:T(8,128)S(1)} fusion(s32[1536]{0:T(1024)} %fusion.35, f32[1536,96]{1,0:T(8,128)} %copy.84, f32[]{:T(128)} %constant.37.clone.1), kind=kCustom, calls=%fused_computation.48 | custom fusion | flops 147456 | bytes 1573376 | tf_op jit(solution)/shard_map/scatter-add | solution.py:33
  322.8 12.2 %scatter_fusion.1 = f32[96,4096]{1,0:T(8,128)} fusion(f32[96,4096]{1,0:T(8,128)} %copy.85, s32[96]{0:T(128)S(1)} %fusion.39, f32[96]{0:T(128)S(1)} %copy-done.42), kind=kCustom, calls=%fused_computation.13 | custom fusion | flops 96 | bytes 1920 | tf_op jit(solution)/shard_map/scatter-add | solution.py:137
  335.0 3.6 collective-permute-done.3
  340.3 36.4 %collective-permute-done.4 = f32[96,4096]{1,0:T(8,128)S(1)} collective-permute-done((f32[96,4096]{1,0:T(8,128)S(1)}, f32[96,4096]{1,0:T(8,128)S(1)}, u32[]{:S(2)}, u32[]{:S(2)}) %collective-permute-start.4) | collective-permute-done | bytes 1572896 | tf_op jit(solution)/shard_map/ppermute | solution.py:142
  377.0 70.2 %collective-permute-done.5 = f32[96,4096]{1,0:T(8,128)S(1)} collective-permute-done((f32[96,4096]{1,0:T(8,128)S(1)}, f32[96,4096]{1,0:T(8,128)S(1)}, u32[]{:S(2)}, u32[]{:S(2)}) %collective-permute-start.5) | collective-permute-done | bytes 1572896 | tf_op jit(solution)/shard_map/ppermute | solution.py:142
  447.2 11.2 %fusion.2 = f32[96,512]{1,0:T(8,128)} fusion(f32[1,512,4096]{2,1,0:T(8,128)} %param.19, f32[96,4096]{1,0:T(8,128)S(1)} %add.274, f32[96,4096]{1,0:T(8,128)S(1)} %collective-permute-done.5), kind=kOutput, calls=%fused_computation.19 | convolution fusion | flops 2416312320 | bytes 11730944 | tf_op jit(solution)/shard_map/dot_general | solution.py:143
  459.3 22.2 %all-gather.8.cloned.1.call-done = f32[96,4096]{1,0:T(8,128)} async-done(((f32[96,512]{1,0:T(8,128)}), f32[96,4096]{1,0:T(8,128)}) %all-gather.8.cloned.1.call-update) | async-done | bytes 1572880 | tf_op jit(solution)/shard_map/all_gather | solution.py:38
  483.4 3.7 gather_fusion.7
  495.2 3.8 all-to-all-start.1
  511.3 4.8 add_reduce_fusion
  516.1 13.1 %all-to-all-done.1 = f32[32,17,288]{2,1,0:T(8,128)} async-done(((f32[32,17,288]{2,1,0:T(8,128)}), f32[32,17,288]{2,1,0:T(8,128)}, u32[]{:S(2)}, u32[]{:S(2)}) %all-to-all-start.1) | async-done | bytes 626720 | tf_op jit(solution)/shard_map/all_to_all | solution.py:121
  540.8 9.7 %scatter_custom_fusion.6 = f32[96,4096]{0,1:T(8,128)S(1)} fusion(s32[1536]{0:T(1024)} %fusion.35, f32[1536,96]{1,0:T(8,128)S(1)} %copy.94, f32[]{:T(128)} %constant.37.clone.1), kind=kCustom, calls=%fused_computation.46 | custom fusion | flops 147456 | bytes 1573376 | tf_op jit(solution)/shard_map/scatter-add | solution.py:33
  552.3 12.2 %scatter_fusion.2 = f32[96,4096]{1,0:T(8,128)} fusion(f32[96,4096]{1,0:T(8,128)} %copy.95, s32[96]{0:T(128)S(1)} %fusion.39, f32[96]{0:T(128)S(1)} %copy-done.41), kind=kCustom, calls=%fused_computation.16 | custom fusion | flops 96 | bytes 1920 | tf_op jit(solution)/shard_map/scatter-add | solution.py:137
  569.8 36.4 %collective-permute-done.7 = f32[96,4096]{1,0:T(8,128)S(1)} collective-permute-done((f32[96,4096]{1,0:T(8,128)S(1)}, f32[96,4096]{1,0:T(8,128)S(1)}, u32[]{:S(2)}, u32[]{:S(2)}) %collective-permute-start.7) | collective-permute-done | bytes 1572896 | tf_op jit(solution)/shard_map/ppermute | solution.py:142
  606.5 70.2 %collective-permute-done.8 = f32[96,4096]{1,0:T(8,128)S(1)} collective-permute-done((f32[96,4096]{1,0:T(8,128)S(1)}, f32[96,4096]{1,0:T(8,128)S(1)}, u32[]{:S(2)}, u32[]{:S(2)}) %collective-permute-start.8) | collective-permute-done | bytes 1572896 | tf_op jit(solution)/shard_map/ppermute | solution.py:142
  676.7 11.2 %fusion = f32[96,512]{1,0:T(8,128)} fusion(f32[1,512,4096]{2,1,0:T(8,128)} %param.19, f32[96,4096]{1,0:T(8,128)S(1)} %add.286, f32[96,4096]{1,0:T(8,128)S(1)} %collective-permute-done.8), kind=kOutput, calls=%fused_computation.17 | convolution fusion | flops 2416312320 | bytes 11730944 | tf_op jit(solution)/shard_map/dot_general | solution.py:143
  687.9 23.1 %all-gather.10.cloned.1.call-done = f32[96,4096]{1,0:T(8,128)} async-done(((f32[96,512]{1,0:T(8,128)}), f32[96,4096]{1,0:T(8,128)}) %all-gather.10.cloned.1.call-update) | async-done | bytes 1572880 | tf_op jit(solution)/shard_map/all_gather | solution.py:38
  712.9 3.7 gather_fusion.8
  (216 shorter events, 150.9 us)
Async XLA Ops:
  7.2 18.6 %copy-start.43 = (s32[96]{0:T(128)S(1)}, s32[96]{0:T(128)}, u32[]{:S(2)}) copy-start(s32[96]{0:T(128)} %param.22) | copy-start | bytes 1156
  7.2 23.8 %copy-start.2 = (f32[1,6,3,96,512]{4,3,2,1,0:T(8,128)S(1)}, f32[1,6,3,96,512]{4,3,2,1,0:T(8,128)}, u32[]{:S(2)}) copy-start(f32[1,6,3,96,512]{4,3,2,1,0:T(8,128)} %param.33) | copy-start | bytes 10616836
  7.2 34.3 %all-gather.12.cloned.1.call-start = ((), (), s32[]{:S(2)}) async-start(), calls=%async_computation.5 | async-start | bytes 2359296 | tf_op jit(solution)/shard_map/all_gather | solution.py:38
  9.2 233.0 %all-gather.6.cloned.1.call-start = ((), (), s32[]{:S(2)}) async-start(), calls=%async_computation.2 | async-start | bytes 1769472 | tf_op jit(solution)/shard_map/all_gather | solution.py:38
  12.5 11.1 %copy-start.31 = (s32[1536]{0:T(1024)}, s32[1536]{0:T(1024)S(1)}, u32[]{:S(2)}) copy-start(s32[1536]{0:T(1024)S(1)} %reshape_squeeze.5) | copy-start | bytes 18436
  20.3 10.7 %copy-start.21 = (f32[6,3,1,512]{3,1,2,0:T(4,128)S(1)}, f32[6,3,1,512]{3,1,2,0:T(4,128)}, u32[]{:S(2)}) copy-start(f32[6,3,1,512]{3,1,2,0:T(4,128)} %copy.124) | copy-start | bytes 110596
  20.3 10.7 %copy-start.27 = (f32[1,6,512]{2,1,0:T(8,128)S(1)}, f32[1,6,512]{2,1,0:T(8,128)}, u32[]{:S(2)}) copy-start(f32[1,6,512]{2,1,0:T(8,128)} %copy.126) | copy-start | bytes 36868
  50.7 7.8 %copy-start = (f32[1,6,3,96,512]{4,3,2,1,0:T(8,128)S(1)}, f32[1,6,3,96,512]{4,3,2,1,0:T(8,128)}, u32[]{:S(2)}) copy-start(f32[1,6,3,96,512]{4,3,2,1,0:T(8,128)} %param.34) | copy-start | bytes 10616836
  93.9 3.6 collective-permute-start
  99.1 36.6 %collective-permute-start.1 = (f32[96,4096]{1,0:T(8,128)S(1)}, f32[96,4096]{1,0:T(8,128)S(1)}, u32[]{:S(2)}, u32[]{:S(2)}) collective-permute-start(f32[96,4096]{1,0:T(8,128)S(1)} %add.257), channel_id=1, source_target_pairs={{0,2},{1,3},{2,0},{3,1},{4,6},{5,7},{6,4},{7,5},{8,10},{9,11},{10,... | collective-permute-start | bytes 4718600 | tf_op jit(solution)/shard_map/ppermute | solution.py:142
  135.9 70.3 %collective-permute-start.2 = (f32[96,4096]{1,0:T(8,128)S(1)}, f32[96,4096]{1,0:T(8,128)S(1)}, u32[]{:S(2)}, u32[]{:S(2)}) collective-permute-start(f32[96,4096]{1,0:T(8,128)S(1)} %add.258), channel_id=1, source_target_pairs={{0,4},{1,5},{2,6},{3,7},{4,0},{5,1},{6,2},{7,3},{8,12},{9,13},{10,... | collective-permute-start | bytes 4718600 | tf_op jit(solution)/shard_map/ppermute | solution.py:142
  265.8 34.1 %all-to-all-start = ((f32[32,17,288]{2,1,0:T(8,128)}), f32[32,17,288]{2,1,0:T(8,128)}, u32[]{:S(2)}, u32[]{:S(2)}) async-start(f32[32,17,288]{2,1,0:T(8,128)} %all_to_all.16), calls=%async_computation | async-start | bytes 2359296 | tf_op jit(solution)/shard_map/all_to_all | solution.py:121
  269.6 211.9 %all-gather.8.cloned.1.call-start = ((), (), s32[]{:S(2)}) async-start(), calls=%async_computation.3 | async-start | bytes 1769472 | tf_op jit(solution)/shard_map/all_gather | solution.py:38
  309.8 11.2 %copy-start.38 = (f32[1,1,512]{2,1,0:T(1,128)S(1)}, f32[1,1,512]{2,1,0:T(1,128)}, u32[]{:S(2)}) copy-start(f32[1,1,512]{2,1,0:T(1,128)} %get-tuple-element.45) | copy-start | bytes 6148
  309.9 12.9 %copy-start.42 = (f32[96]{0:T(128)S(1)}, f32[96]{0:T(128)}, u32[]{:S(2)}) copy-start(f32[96]{0:T(128)} %multiply_select_fusion.1) | copy-start | bytes 1156
  335.0 3.6 collective-permute-start.3
  340.3 36.5 %collective-permute-start.4 = (f32[96,4096]{1,0:T(8,128)S(1)}, f32[96,4096]{1,0:T(8,128)S(1)}, u32[]{:S(2)}, u32[]{:S(2)}) collective-permute-start(f32[96,4096]{1,0:T(8,128)S(1)} %add.273), channel_id=1, source_target_pairs={{0,2},{1,3},{2,0},{3,1},{4,6},{5,7},{6,4},{7,5},{8,10},{9,11},{10,... | collective-permute-start | bytes 4718600 | tf_op jit(solution)/shard_map/ppermute | solution.py:142
  376.9 81.5 %copy-start.14 = (f32[3,96,512]{2,1,0:T(8,128)S(1)}, f32[3,96,512]{2,1,0:T(8,128)}, u32[]{:S(2)}) copy-start(f32[3,96,512]{2,1,0:T(8,128)} %get-tuple-element.3) | copy-start | bytes 1769476
  376.9 70.3 %collective-permute-start.5 = (f32[96,4096]{1,0:T(8,128)S(1)}, f32[96,4096]{1,0:T(8,128)S(1)}, u32[]{:S(2)}, u32[]{:S(2)}) collective-permute-start(f32[96,4096]{1,0:T(8,128)S(1)} %add.274), channel_id=1, source_target_pairs={{0,4},{1,5},{2,6},{3,7},{4,0},{5,1},{6,2},{7,3},{8,12},{9,13},{10,... | collective-permute-start | bytes 4718600 | tf_op jit(solution)/shard_map/ppermute | solution.py:142
  458.4 25.0 %copy-start.29 = (s32[2048]{0:T(1024)S(1)}, s32[2048]{0:T(1024)}, u32[]{:S(2)}) copy-start(s32[2048]{0:T(1024)} %pad_clamp_fusion) | copy-start | bytes 24580
  483.4 5.4 copy-start.34
  492.7 18.6 %copy-start.1 = (f32[1,6,3,96,512]{4,3,2,1,0:T(8,128)S(1)}, f32[1,6,3,96,512]{4,3,2,1,0:T(8,128)}, u32[]{:S(2)}) copy-start(f32[1,6,3,96,512]{4,3,2,1,0:T(8,128)} %param.34) | copy-start | bytes 10616836
  495.2 34.1 %all-to-all-start.1 = ((f32[32,17,288]{2,1,0:T(8,128)}), f32[32,17,288]{2,1,0:T(8,128)}, u32[]{:S(2)}, u32[]{:S(2)}) async-start(f32[32,17,288]{2,1,0:T(8,128)} %all_to_all.19), calls=%async_computation.1 | async-start | bytes 2359296 | tf_op jit(solution)/shard_map/all_to_all | solution.py:121
  499.0 212.0 %all-gather.10.cloned.1.call-start = ((), (), s32[]{:S(2)}) async-start(), calls=%async_computation.4 | async-start | bytes 1769472 | tf_op jit(solution)/shard_map/all_gather | solution.py:38
  511.3 19.4 %copy-start.35 = (s32[1024]{0:T(1024)S(1)}, s32[1024]{0:T(1024)}, u32[]{:S(2)}) copy-start(s32[1024]{0:T(1024)} %pad_clamp_fusion.1) | copy-start | bytes 12292
  539.7 10.8 %copy-start.37 = (f32[1,1,512]{2,1,0:T(1,128)S(1)}, f32[1,1,512]{2,1,0:T(1,128)}, u32[]{:S(2)}) copy-start(f32[1,1,512]{2,1,0:T(1,128)} %get-tuple-element.43) | copy-start | bytes 6148
  540.5 11.8 %copy-start.41 = (f32[96]{0:T(128)S(1)}, f32[96]{0:T(128)}, u32[]{:S(2)}) copy-start(f32[96]{0:T(128)} %multiply_select_fusion) | copy-start | bytes 1156
  564.5 3.6 collective-permute-start.6
  569.8 36.5 %collective-permute-start.7 = (f32[96,4096]{1,0:T(8,128)S(1)}, f32[96,4096]{1,0:T(8,128)S(1)}, u32[]{:S(2)}, u32[]{:S(2)}) collective-permute-start(f32[96,4096]{1,0:T(8,128)S(1)} %add.285), channel_id=1, source_target_pairs={{0,2},{1,3},{2,0},{3,1},{4,6},{5,7},{6,4},{7,5},{8,10},{9,11},{10,... | collective-permute-start | bytes 4718600 | tf_op jit(solution)/shard_map/ppermute | solution.py:142
  606.4 70.3 %collective-permute-start.8 = (f32[96,4096]{1,0:T(8,128)S(1)}, f32[96,4096]{1,0:T(8,128)S(1)}, u32[]{:S(2)}, u32[]{:S(2)}) collective-permute-start(f32[96,4096]{1,0:T(8,128)S(1)} %add.286), channel_id=1, source_target_pairs={{0,4},{1,5},{2,6},{3,7},{4,0},{5,1},{6,2},{7,3},{8,12},{9,13},{10,... | collective-permute-start | bytes 4718600 | tf_op jit(solution)/shard_map/ppermute | solution.py:142
  687.9 24.9 %copy-start.30 = (s32[2048]{0:T(1024)S(1)}, s32[2048]{0:T(1024)}, u32[]{:S(2)}) copy-start(s32[2048]{0:T(1024)} %pad_clamp_fusion) | copy-start | bytes 24580
  712.8 5.4 copy-start.8
  (28 other events, 62.5 us)
Sparse Core Ops, SparseCore 0:
  9.6 31.8 all-gather.11
  217.5 24.6 all-gather.5
  458.6 22.9 all-gather.7
  688.0 22.9 all-gather.9
